TPU v7x, 256 devices: a whole 4x4x8 slice. The times are simulated.
256 devices in a mesh: view: 8 (over x, core), gauss: 32 (over y, z).
Axes of the slice: x: 4, y: 4, z: 8, core: 2. Of those that a mesh axis runs over, the one named last changes fastest.
Arguments:
- means: float32 [3, 524288], P(None, 'gauss'), may hold values from -1 to 1
- scales: float32 [3, 524288], P(None, 'gauss'), may hold values from 0.05 to 0.6
- quats: float32 [4, 524288], P(None, 'gauss'), may hold values from -6 to 6
- attrs: float32 [49, 524288], P(None, 'gauss'), may hold values from -6 to 6
- grad_screen: float32 [32, 2, 524288], P('view', None, 'gauss'), may hold values from -6 to 6
- visible: int32 [32, 524288], P('view', 'gauss'), may hold values 0 or 1
- clone_mask: int32 [524288], P('gauss'), may hold values from 0 to 1, as said below
- rotation: float32 [32, 3, 3], P('view'), may hold values from -3.5 to 3.5
- shift: float32 [32, 3], P('view'), may hold values from 2 to 5
- focal: float32 [32], P('view'), may hold values from 1 to 4
Outputs:
- peak_stats: float32 [2, 524288], P(None, 'gauss')
- clones: float32 [61, 524288], P(None, 'gauss')
- clone_total: int32 [], replicated
Inputs may be any that keep to these rules, and one draw needn't show every extreme that they name: `clone_mask`: in every draw some shard of 16384 consecutive Gaussians has all of them marked.
All inputs are finite; a program needn't handle non-finite values. No bound on the sum of `visible` on one device may be relied on, other than what follows from the above.
Results may differ from a plain program's by a relative error of at most 0.0003.
Values sent between devices are 32-bit elements; how exact they have to be, the bound alone decides.
No kernel may reach another device: no remote copies, remote signals or barrier semaphores. Data moves between devices by JAX's collectives and lax.ppermute only.
A program may use at most 128 MiB of HBM per device.

v0:
```python
import jax
import jax.numpy as jnp
from jax import lax
from jax.sharding import PartitionSpec as P

G_DEV = 16384


def copy_for_each(x, axis):
    count = lax.axis_size(axis)
    return lax.all_to_all(jnp.broadcast_to(x[None], (count, *x.shape)), axis, 0, 0, tiled=True)


def of_everyone(x, axis):
    return copy_for_each(x, axis).max(axis=0)


def together(arrays, axis):
    vector, at, done = (jnp.concatenate([a.reshape(-1) for a in arrays]), 0, [])
    running = of_everyone(vector, axis)
    for a in arrays:
        done.append(running[at : at + a.size].reshape(a.shape))
        at += a.size
    return tuple(done)


def folded_in_pairs(pieces, combine):
    while len(jax.tree.leaves(pieces)[0]) > 1:
        pieces = jax.vmap(combine)(*(pieces[side::2] for side in (0, 1)))
    return pieces[0]


def prefix(x, axis, combine, identity):
    count, mine = (lax.axis_size(axis), lax.axis_index(axis))
    passed = jnp.arange(count) < mine

    def kept(part, zero, own):
        part = jnp.where(
            passed.reshape(-1, *(1 for _ in own.shape)), part, jnp.asarray(zero, own.dtype)
        )
        return part

    pieces = copy_for_each(x, axis)
    return folded_in_pairs(kept(pieces, identity, x), combine)


def of_everyone_2(x, axis):
    everything = copy_for_each(x, axis)
    return jnp.sum(everything, axis=0)


def quat_factor(scales, quats):
    inv = 1.0 / jnp.sqrt(jnp.sum(quats * quats, axis=0) + 0.25)
    w, x, y, z = (quats[0] * inv, quats[1] * inv, quats[2] * inv, quats[3] * inv)
    rq = [
        [1 - 2 * (y * y + z * z), 2 * (x * y - w * z), 2 * (x * z + w * y)],
        [2 * (x * y + w * z), 1 - 2 * (x * x + z * z), 2 * (y * z - w * x)],
        [2 * (x * z - w * y), 2 * (y * z + w * x), 1 - 2 * (x * x + y * y)],
    ]
    return [[rq[i][j] * scales[j] for j in range(3)] for i in range(3)]


def view_stats(means, factor, grad, seen, rot, trans, focal_v):
    point = [
        rot[i, 0] * means[0] + rot[i, 1] * means[1] + rot[i, 2] * means[2] + trans[i]
        for i in range(3)
    ]
    depth = jnp.maximum(point[2], 1.0)
    j00 = focal_v / depth
    j02 = -focal_v * point[0] / (depth * depth)
    j12 = -focal_v * point[1] / (depth * depth)
    first = [j00 * rot[0, j] + j02 * rot[2, j] for j in range(3)]
    second = [j00 * rot[1, j] + j12 * rot[2, j] for j in range(3)]
    prow = [sum((first[j] * factor[j][k] for j in range(3))) for k in range(3)]
    qrow = [sum((second[j] * factor[j][k] for j in range(3))) for k in range(3)]
    a_val = prow[0] ** 2 + prow[1] ** 2 + prow[2] ** 2 + 0.3
    c_val = qrow[0] ** 2 + qrow[1] ** 2 + qrow[2] ** 2 + 0.3
    b_val = prow[0] * qrow[0] + prow[1] * qrow[1] + prow[2] * qrow[2]
    half = 0.5 * (a_val - c_val)
    lam = 0.5 * (a_val + c_val) + jnp.sqrt(half * half + b_val * b_val + 0.01)
    seenf = seen.astype(jnp.float32)
    radius = 3.0 * jnp.sqrt(lam) * seenf
    gnorm = jnp.sqrt(grad[0] * grad[0] + grad[1] * grad[1]) * seenf
    return (gnorm, radius)


def add_ints(earlier, later):
    return earlier + later


def body(means, scales, quats, attrs, grad_screen, visible, clone_mask, rotation, shift, focal):
    factor = quat_factor(scales, quats)
    gmax = jnp.zeros(means.shape[1], jnp.float32)
    rmax = jnp.zeros(means.shape[1], jnp.float32)
    for v in range(grad_screen.shape[0]):
        gnorm, radius = view_stats(
            means, factor, grad_screen[v], visible[v], rotation[v], shift[v], focal[v]
        )
        gmax = jnp.maximum(gmax, gnorm)
        rmax = jnp.maximum(rmax, radius)
    gmax, rmax = together((gmax, rmax), "view")
    peak = jnp.stack([gmax, rmax])
    rows = jnp.concatenate([means, scales, quats, attrs, peak], axis=0)
    feat_rows = rows.shape[0]
    shards = lax.axis_size("gauss")
    cap_blk = G_DEV // 128
    count = jnp.sum(clone_mask)
    blocks = (count + 127) // 128
    offset = prefix(blocks, "gauss", add_ints, jnp.int32(0))
    summed = of_everyone_2(count.astype(jnp.float32), "gauss")
    total = summed.astype(jnp.int32)
    rank = jnp.cumsum(clone_mask) - 1
    where_to = jnp.where(clone_mask == 1, rank, cap_blk * 128)
    packed = (
        jnp.zeros((feat_rows, cap_blk * 128), jnp.float32).at[:, where_to].set(rows, mode="drop")
    )
    packed = packed.reshape(feat_rows, cap_blk, 128)
    per = (cap_blk + shards - 1) // shards
    target = jnp.arange(shards, dtype=jnp.int32)[:, None]
    within = jnp.arange(per, dtype=jnp.int32)[None, :]
    local_blk = (target - offset) % shards + within * shards
    valid = local_blk < blocks
    picked = jnp.minimum(local_blk, cap_blk - 1).reshape(-1)
    outgoing = packed[:, picked, :] * valid.reshape(1, -1, 1).astype(jnp.float32)
    outgoing = outgoing.reshape(feat_rows, shards, per, 128)
    slot_ids = (
        jnp.where(valid, (offset + local_blk) // shards, cap_blk)
        .astype(jnp.int32)
        .reshape(1, shards, per)
    )
    width = 128 // lax.axis_size("view")
    start = lax.axis_index("view") * width
    portion = lax.dynamic_slice_in_dim(outgoing, start, width, 3)
    arrived, slots_in = (
        lax.all_to_all(portion, "gauss", split_axis=1, concat_axis=1, tiled=True),
        lax.all_to_all(slot_ids, "gauss", split_axis=1, concat_axis=1, tiled=True),
    )
    arrived = arrived.reshape(feat_rows, shards * per, width)
    partial_place = (
        jnp.zeros((feat_rows, cap_blk, width), jnp.float32)
        .at[:, slots_in.reshape(-1)]
        .set(arrived, mode="drop")
    )
    placed = lax.all_gather(partial_place, "view", axis=2, tiled=True)
    clones = placed.reshape(feat_rows, cap_blk * 128)
    return (peak, clones, total)


def solution(mesh):
    return jax.shard_map(
        body,
        mesh=mesh,
        in_specs=(
            P(None, "gauss"),
            P(None, "gauss"),
            P(None, "gauss"),
            P(None, "gauss"),
            P("view", None, "gauss"),
            P("view", "gauss"),
            P("gauss"),
            P("view", None, None),
            P("view", None),
            P("view"),
        ),
        out_specs=(P(None, "gauss"), P(None, "gauss"), P()),
        check_vma=False,
    )
```

profile of v0, /device:TPU:1, one launch (start us, length us, event | category | flops | bytes accessed | tf_op | source)
XLA Modules:
  0.0 326.7 jit_solution(10295088173397887772)
XLA Ops:
  8.9 2.1 compare_select_fusion
  12.2 12.0 %all-to-all-start.1 = ((s32[32,1,1]{2,1,0:T(1,128)}), s32[32,1,1]{2,1,0:T(1,128)S(1)}, u32[]{:S(2)}, u32[]{:S(2)}) async-start(s32[32,1,1]{2,1,0:T(1,128)} %broadcast_in_dim.45), calls=%async_computation.1 | async-start | bytes 32768 | tf_op jit(solution)/shard_map/all_to_all | solution.py:11
  24.2 2.4 fusion.6
  29.9 1.8 fusion.11
  33.8 7.2 %multiply_add_fusion.23 = (f32[1,16384]{1,0:T(1,128)S(1)}, f32[1,16384]{1,0:T(1,128)S(1)}, f32[1,16384]{1,0:T(1,128)S(1)}, f32[1,16384]{1,0:T(1,128)S(1)}) fusion(f32[]{:T(128)} %bitcast.13, f32[]{:T(128)} %bitcast.9, f32[]{:T(128)} %bitcast.16, f32[3,16384]{1,0:T(4,128)} %param.10, f32[]{:T(128)} %bitcast.15, f32[]{:T(128)} %bitcast.14, f32[]{:T(128)S(6)} %neg.16, ...), kind=kLoop, calls=%fused_computation.35 | loop fusion | flops 327680 | bytes 458792 | tf_op jit(solution)/shard_map/add | solution.py:72
  41.1 7.3 %multiply_add_fusion.22 = (f32[1,16384]{1,0:T(1,128)S(1)}, f32[1,16384]{1,0:T(1,128)S(1)}, f32[1,16384]{1,0:T(1,128)S(1)}, f32[1,16384]{1,0:T(1,128)S(1)}) fusion(f32[1,16384]{1,0:T(1,128)S(1)} %get-tuple-element.22, f32[1,16384]{1,0:T(1,128)S(1)} %get-tuple-element.23, f32[]{:T(128)} %bitcast.14, f32[]{:T(128)} %bitcast.10, f32[]{:T(128)} %bitcast.11, ...), kind=kLoop, calls=%fused_computation.34 | loop fusion | flops 294912 | bytes 655400 | tf_op jit(solution)/shard_map/add | solution.py:72
  48.3 2.5 multiply_add_fusion.19
  52.2 7.4 %multiply_add_fusion.17 = (f32[1,16384]{1,0:T(1,128)S(1)}, f32[1,16384]{1,0:T(1,128)S(1)}, f32[1,16384]{1,0:T(1,128)S(1)}, f32[1,16384]{1,0:T(1,128)S(1)}) fusion(f32[]{:T(128)} %bitcast.39, f32[]{:T(128)} %bitcast.35, f32[]{:T(128)} %bitcast.42, f32[3,16384]{1,0:T(4,128)} %param.10, f32[]{:T(128)} %bitcast.41, f32[]{:T(128)} %bitcast.40, f32[]{:T(128)S(6)} %neg.17, ...), kind=kLoop, calls=%fused_computation.29 | loop fusion | flops 327680 | bytes 458792 | tf_op jit(solution)/shard_map/add | solution.py:72
  59.6 7.2 %multiply_add_fusion.16 = (f32[1,16384]{1,0:T(1,128)S(1)}, f32[1,16384]{1,0:T(1,128)S(1)}, f32[1,16384]{1,0:T(1,128)S(1)}, f32[1,16384]{1,0:T(1,128)S(1)}) fusion(f32[1,16384]{1,0:T(1,128)S(1)} %get-tuple-element.28, f32[1,16384]{1,0:T(1,128)S(1)} %get-tuple-element.29, f32[]{:T(128)} %bitcast.40, f32[]{:T(128)} %bitcast.36, f32[]{:T(128)} %bitcast.37, ...), kind=kLoop, calls=%fused_computation.28 | loop fusion | flops 294912 | bytes 655400 | tf_op jit(solution)/shard_map/add | solution.py:72
  66.8 2.5 multiply_add_fusion.13
  70.7 7.4 %multiply_add_fusion.11 = (f32[1,16384]{1,0:T(1,128)S(1)}, f32[1,16384]{1,0:T(1,128)S(1)}, f32[1,16384]{1,0:T(1,128)S(1)}, f32[1,16384]{1,0:T(1,128)S(1)}) fusion(f32[]{:T(128)} %bitcast.58, f32[]{:T(128)} %bitcast.54, f32[]{:T(128)} %bitcast.61, f32[3,16384]{1,0:T(4,128)} %param.10, f32[]{:T(128)} %bitcast.60, f32[]{:T(128)} %bitcast.59, f32[]{:T(128)S(6)} %neg.18, ...), kind=kLoop, calls=%fused_computation.23 | loop fusion | flops 327680 | bytes 458792 | tf_op jit(solution)/shard_map/add | solution.py:72
  78.1 7.4 %multiply_add_fusion.10 = (f32[1,16384]{1,0:T(1,128)S(1)}, f32[1,16384]{1,0:T(1,128)S(1)}, f32[1,16384]{1,0:T(1,128)S(1)}, f32[1,16384]{1,0:T(1,128)S(1)}) fusion(f32[1,16384]{1,0:T(1,128)S(1)} %get-tuple-element.34, f32[1,16384]{1,0:T(1,128)S(1)} %get-tuple-element.35, f32[]{:T(128)} %bitcast.59, f32[]{:T(128)} %bitcast.55, f32[]{:T(128)} %bitcast.56, ...), kind=kLoop, calls=%fused_computation.22 | loop fusion | flops 294912 | bytes 655400 | tf_op jit(solution)/shard_map/add | solution.py:72
  85.4 2.6 multiply_add_fusion.7
  89.4 7.4 %multiply_add_fusion.5 = (f32[1,16384]{1,0:T(1,128)S(1)}, f32[1,16384]{1,0:T(1,128)S(1)}, f32[1,16384]{1,0:T(1,128)S(1)}, f32[1,16384]{1,0:T(1,128)S(1)}) fusion(f32[]{:T(128)} %bitcast.77, f32[]{:T(128)} %bitcast.73, f32[]{:T(128)} %bitcast.80, f32[3,16384]{1,0:T(4,128)} %param.10, f32[]{:T(128)} %bitcast.79, f32[]{:T(128)} %bitcast.78, f32[]{:T(128)S(6)} %neg.19, ...), kind=kLoop, calls=%fused_computation.17 | loop fusion | flops 327680 | bytes 458792 | tf_op jit(solution)/shard_map/add | solution.py:72
  96.8 7.4 %multiply_add_fusion.4 = (f32[1,16384]{1,0:T(1,128)S(1)}, f32[1,16384]{1,0:T(1,128)S(1)}, f32[1,16384]{1,0:T(1,128)S(1)}, f32[1,16384]{1,0:T(1,128)S(1)}) fusion(f32[1,16384]{1,0:T(1,128)S(1)} %get-tuple-element.40, f32[1,16384]{1,0:T(1,128)S(1)} %get-tuple-element.41, f32[]{:T(128)} %bitcast.78, f32[]{:T(128)} %bitcast.74, f32[]{:T(128)} %bitcast.75, ...), kind=kLoop, calls=%fused_computation.16 | loop fusion | flops 294912 | bytes 655400 | tf_op jit(solution)/shard_map/add | solution.py:72
  104.2 2.6 multiply_add_fusion.1
  110.2 1.8 multiply_maximum_fusion
  113.5 5.3 %all-to-all-start = ((f32[8,1,32768]{2,1,0:T(1,128)}), f32[8,1,32768]{2,1,0:T(1,128)S(1)}, u32[]{:S(2)}, u32[]{:S(2)}) async-start(f32[8,1,32768]{2,1,0:T(1,128)} %broadcast_in_dim.24), calls=%async_computation | async-start | bytes 2097152 | tf_op jit(solution)/shard_map/all_to_all | solution.py:11
  125.2 8.5 %all-to-all-done = f32[8,1,32768]{2,1,0:T(1,128)S(1)} async-done(((f32[8,1,32768]{2,1,0:T(1,128)}), f32[8,1,32768]{2,1,0:T(1,128)S(1)}, u32[]{:S(2)}, u32[]{:S(2)}) %all-to-all-start) | async-done | bytes 1048608 | tf_op jit(solution)/shard_map/all_to_all | solution.py:11
  133.7 9.7 %all-to-all-start.2 = ((s32[1,32,4]{2,0,1:T(1,128)}), s32[1,32,4]{2,0,1:T(1,128)S(1)}, u32[]{:S(2)}, u32[]{:S(2)}) async-start(s32[1,32,4]{2,0,1:T(1,128)} %compare_select_fusion.1), calls=%async_computation.2 | async-start | bytes 32768 | tf_op jit(solution)/shard_map/all_to_all | solution.py:136
  144.2 21.5 %concatenate.8 = f32[61,16384]{1,0:T(8,128)} concatenate(f32[3,16384]{1,0:T(4,128)S(1)} %copy-done.1, f32[3,16384]{1,0:T(4,128)S(1)} %copy-done.3, f32[4,16384]{1,0:T(4,128)S(1)} %copy-done.2, f32[49,16384]{1,0:T(8,128)} %param.13, f32[1,16384]{1,0:T(1,128)S(1)} %bitcast.129, f32[1,16384]{1,0:T(1,128)S(1)} %bitcast.131), dimensions={0} | concatenate | bytes 7995392 | tf_op jit(solution)/shard_map/concatenate | solution.py:103
  165.8 6.9 %copy.40 = f32[16384,61]{1,0:T(8,128)} copy(f32[16384,61]{0,1:T(8,128)} %bitcast.126) | data formatting | bytes 7995392 | tf_op jit(solution)/shard_map/concatenate | solution.py:103
  172.7 44.3 %scatter_custom_fusion = f32[61,16384]{0,1:T(8,128)} fusion(s32[16384]{0:T(1024)} %get-tuple-element.78, f32[16384,61]{1,0:T(8,128)} %copy.40, f32[]{:T(128)} %constant.32.clone.1), kind=kCustom, calls=%fused_computation.3 | custom fusion | bytes 3998208 | tf_op jit(solution)/shard_map/scatter | solution.py:115
  217.0 7.7 %gather_fusion = f32[128,61,128]{1,2,0:T(8,128)} fusion(f32[61,128,128]{0,2,1:T(8,128)} %bitcast.125, s32[1024]{0:T(1024)S(1)} %pad_clamp_fusion), kind=kCustom, calls=%fused_computation | custom fusion | bytes 7995904 | tf_op jit(solution)/shard_map/gather | solution.py:124
  226.2 2.3 reshape.640
  228.5 9.1 %all-to-all-start.3 = ((f32[32,1,3904]{2,1,0:T(1,128)}), f32[32,1,3904]{2,1,0:T(1,128)S(1)}, u32[]{:S(2)}, u32[]{:S(2)}) async-start(f32[32,1,3904]{2,1,0:T(1,128)} %reshape.640), calls=%async_computation.3 | async-start | bytes 1015808 | tf_op jit(solution)/shard_map/all_to_all | solution.py:135
  238.9 11.3 %all-to-all-done.3 = f32[32,1,3904]{2,1,0:T(1,128)S(1)} async-done(((f32[32,1,3904]{2,1,0:T(1,128)}), f32[32,1,3904]{2,1,0:T(1,128)S(1)}, u32[]{:S(2)}, u32[]{:S(2)}) %all-to-all-start.3) | async-done | bytes 499744 | tf_op jit(solution)/shard_map/all_to_all | solution.py:135
  250.8 1.8 reduce.9
  254.2 4.5 %scatter_fusion = f32[61,128,16]{0,2,1:T(8,128)S(1)} fusion(f32[61,128,16]{0,2,1:T(8,128)S(1)} %broadcast_in_dim.44, s32[128]{0:T(128)S(1)} %fusion.4, f32[128,61,16]{1,2,0:T(8,128)S(1)} %bitcast.124), kind=kCustom, calls=%fused_computation.2 | custom fusion | bytes 1499648 | tf_op jit(solution)/shard_map/scatter | solution.py:142
  260.3 16.9 %all_to_all.31 = f32[32,1,1]{2,1,0:T(1,128)S(1)} all-to-all(f32[32,1,1]{2,1,0:T(1,128)S(1)} %broadcast_in_dim.51), channel_id=1, replica_groups=mesh['view'=8,'gauss'=32] {'gauss'}, dimensions={0} | all-to-all | bytes 256 | tf_op jit(solution)/shard_map/all_to_all | solution.py:11
  279.3 32.5 %all-gather.2.cloned.1.call-done = f32[61,128,128]{0,2,1:T(8,128)} async-done(((f32[61,128,16]{0,2,1:T(8,128)}), f32[61,128,128]{0,2,1:T(8,128)}) %all-gather.2.cloned.1.call-update) | async-done | bytes 3997712 | tf_op jit(solution)/shard_map/all_gather | solution.py:144
  311.8 6.8 %copy.42 = f32[61,16384]{1,0:T(8,128)} copy(f32[61,16384]{0,1:T(8,128)} %bitcast.127) | data formatting | bytes 7995392
  (74 shorter events, 27.1 us)
Async XLA Ops:
  7.2 101.4 %copy-start.3 = (f32[3,16384]{1,0:T(4,128)S(1)}, f32[3,16384]{1,0:T(4,128)}, u32[]{:S(2)}) copy-start(f32[3,16384]{1,0:T(4,128)} %param.11) | copy-start | bytes 589828
  7.2 102.1 %copy-start.4 = (f32[4,2,16384]{2,1,0:T(2,128)S(1)}, f32[4,2,16384]{2,1,0:T(2,128)}, u32[]{:S(2)}) copy-start(f32[4,2,16384]{2,1,0:T(2,128)} %param.14) | copy-start | bytes 1572868
  12.2 99.8 %all-to-all-start.1 = ((s32[32,1,1]{2,1,0:T(1,128)}), s32[32,1,1]{2,1,0:T(1,128)S(1)}, u32[]{:S(2)}, u32[]{:S(2)}) async-start(s32[32,1,1]{2,1,0:T(1,128)} %broadcast_in_dim.45), calls=%async_computation.1 | async-start | bytes 32768 | tf_op jit(solution)/shard_map/all_to_all | solution.py:11
  24.2 120.0 %copy-start.1 = (f32[3,16384]{1,0:T(4,128)S(1)}, f32[3,16384]{1,0:T(4,128)}, u32[]{:S(2)}) copy-start(f32[3,16384]{1,0:T(4,128)} %param.10) | copy-start | bytes 589828
  24.2 120.0 %copy-start.2 = (f32[4,16384]{1,0:T(4,128)S(1)}, f32[4,16384]{1,0:T(4,128)}, u32[]{:S(2)}) copy-start(f32[4,16384]{1,0:T(4,128)} %param.12) | copy-start | bytes 786436
  113.5 20.2 %all-to-all-start = ((f32[8,1,32768]{2,1,0:T(1,128)}), f32[8,1,32768]{2,1,0:T(1,128)S(1)}, u32[]{:S(2)}, u32[]{:S(2)}) async-start(f32[8,1,32768]{2,1,0:T(1,128)} %broadcast_in_dim.24), calls=%async_computation | async-start | bytes 2097152 | tf_op jit(solution)/shard_map/all_to_all | solution.py:11
  133.7 94.8 %all-to-all-start.2 = ((s32[1,32,4]{2,0,1:T(1,128)}), s32[1,32,4]{2,0,1:T(1,128)S(1)}, u32[]{:S(2)}, u32[]{:S(2)}) async-start(s32[1,32,4]{2,0,1:T(1,128)} %compare_select_fusion.1), calls=%async_computation.2 | async-start | bytes 32768 | tf_op jit(solution)/shard_map/all_to_all | solution.py:136
  228.5 21.8 %all-to-all-start.3 = ((f32[32,1,3904]{2,1,0:T(1,128)}), f32[32,1,3904]{2,1,0:T(1,128)S(1)}, u32[]{:S(2)}, u32[]{:S(2)}) async-start(f32[32,1,3904]{2,1,0:T(1,128)} %reshape.640), calls=%async_computation.3 | async-start | bytes 1015808 | tf_op jit(solution)/shard_map/all_to_all | solution.py:135
  237.6 74.3 %all-gather.2.cloned.1.call-start = ((), (), s32[]{:S(2)}) async-start(), calls=%async_computation.5 | async-start | bytes 9437184 | tf_op jit(solution)/shard_map/all_gather | solution.py:144
  258.8 1.0 copy-start
Sparse Core Ops, SparseCore 0:
  259.9 51.9 all-gather.1
where the time goes:
time: 329 us; the launch traced here: 327 us
  local copies, waits for them, and re-layouts  113 us (34%)
  other arithmetic  87.1 us (26%)
  waiting for transfers between devices  52.4 us (16%)
  starting transfers between devices  36.1 us (11%)
  between operations  21.3 us (6%)
  blocking collectives  16.9 us (5%)
    add x8, other arithmetic, view_stats(): first = [j00 * rot[0, j] + j02 * rot[2, j] for j in range(3)]  58.6 us
    scatter x1, local copies, waits for them, and re-layouts, body(): jnp.zeros((feat_rows, cap_blk * 128), jnp.float32).at[:, where_to]  44.3 us
    all_gather x1, waiting for transfers between devices, body(): placed = lax.all_gather(partial_place, 'view', axis=2, tiled=True)  32.5 us
    concatenate x2, local copies, waits for them, and re-layouts, body(): rows = jnp.concatenate([means, scales, quats, attrs, peak], axis=0)  28.5 us
    all_to_all x2, starting transfers between devices, copy_for_each(): lax.all_to_all(jnp.broadcast_to(x[None], (count, *x.shape)), axis, 0, 0,...  17.3 us
    all_to_all x1, blocking collectives, copy_for_each(): lax.all_to_all(jnp.broadcast_to(x[None], (count, *x.shape)), axis, 0, 0,...  16.9 us
    unnamed x15, local copies, waits for them, and re-layouts  11.7 us
    all_to_all x1, waiting for transfers between devices, body(): lax.all_to_all(portion, 'gauss', split_axis=1, concat_axis=1, tiled=True)  11.3 us
  transfers between devices with their start and end apart: 5, of which 3 were waited for; matrix products, arithmetic and copies ran while one was open for 54% of the time, Pallas kernels for 0%

commit v1 on v0

--- a/solution.py
+++ b/solution.py
@@ -141,7 +141,7 @@
         .at[:, slots_in.reshape(-1)]
         .set(arrived, mode="drop")
     )
-    placed = lax.all_gather(partial_place, "view", axis=2, tiled=True)
+    placed = jnp.concatenate(lax.all_gather(partial_place, "view"), axis=2)
     clones = placed.reshape(feat_rows, cap_blk * 128)
     return (peak, clones, total)
 

time: 329 us -> 320 us (0.973)
  waiting for transfers between devices: 52.4 us -> 34.1 us
  local copies, waits for them, and re-layouts: 113 us -> 122 us
    all_gather x1, waiting for transfers between devices: 32.5 us -> 14 us  [body(): placed = jnp.concatenate(lax.all_gather(partial_place, 'view'), axis=2)]
    reshape x1 -> x2, local copies, waits for them, and re-layouts: 1 us -> 10.3 us  [the longest x1 9.25 us: body(): placed = jnp.concatenate(lax.all_gather(partial_place, 'view'), axis=2)]
    unnamed x15 -> x13, local copies, waits for them, and re-layouts: 11.7 us -> 10.7 us
  transfers between devices with their start and end apart: 5 -> 5, of which waited for: 3 -> 3; matrix products, arithmetic and copies ran while one was open for 54% -> 56% of each run, Pallas kernels for 0% -> 0%
where the time goes in v1:
time: 320 us; the launch traced here: 318 us
  local copies, waits for them, and re-layouts  122 us (38%)
  other arithmetic  87 us (27%)
  starting transfers between devices  36.1 us (11%)
  waiting for transfers between devices  34.1 us (11%)
  between operations  21.1 us (7%)
  blocking collectives  16.9 us (5%)
    add x8, other arithmetic, view_stats(): first = [j00 * rot[0, j] + j02 * rot[2, j] for j in range(3)]  58.4 us
    scatter x1, local copies, waits for them, and re-layouts, body(): jnp.zeros((feat_rows, cap_blk * 128), jnp.float32).at[:, where_to]  44.3 us
    concatenate x2, local copies, waits for them, and re-layouts, body(): rows = jnp.concatenate([means, scales, quats, attrs, peak], axis=0)  28.5 us
    all_to_all x2, starting transfers between devices, copy_for_each(): lax.all_to_all(jnp.broadcast_to(x[None], (count, *x.shape)), axis, 0, 0,...  17.3 us
    all_to_all x1, blocking collectives, copy_for_each(): lax.all_to_all(jnp.broadcast_to(x[None], (count, *x.shape)), axis, 0, 0,...  16.9 us
    all_gather x1, waiting for transfers between devices, body(): placed = jnp.concatenate(lax.all_gather(partial_place, 'view'), axis=2)  14 us
    all_to_all x1, waiting for transfers between devices, body(): lax.all_to_all(portion, 'gauss', split_axis=1, concat_axis=1, tiled=True)  11.3 us
    unnamed x13, local copies, waits for them, and re-layouts  10.7 us
  transfers between devices with their start and end apart: 5, of which 3 were waited for; matrix products, arithmetic and copies ran while one was open for 56% of the time, Pallas kernels for 0%

profile of v1, /device:TPU:1, one launch (start us, length us, event | category | flops | bytes accessed | tf_op | source)
XLA Modules:
  0.0 317.6 jit_solution(1975091034847332997)
XLA Ops:
  8.9 2.2 compare_select_fusion
  12.3 12.0 %all-to-all-start.1 = ((s32[32,1,1]{2,1,0:T(1,128)}), s32[32,1,1]{2,1,0:T(1,128)S(1)}, u32[]{:S(2)}, u32[]{:S(2)}) async-start(s32[32,1,1]{2,1,0:T(1,128)} %broadcast_in_dim.45), calls=%async_computation.1 | async-start | bytes 32768 | tf_op jit(solution)/shard_map/all_to_all | solution.py:11
  24.4 2.4 fusion.6
  30.0 1.8 fusion.11
  33.8 7.2 %multiply_add_fusion.23 = (f32[1,16384]{1,0:T(1,128)S(1)}, f32[1,16384]{1,0:T(1,128)S(1)}, f32[1,16384]{1,0:T(1,128)S(1)}, f32[1,16384]{1,0:T(1,128)S(1)}) fusion(f32[]{:T(128)} %bitcast.13, f32[]{:T(128)} %bitcast.9, f32[]{:T(128)} %bitcast.16, f32[3,16384]{1,0:T(4,128)} %param.10, f32[]{:T(128)} %bitcast.15, f32[]{:T(128)} %bitcast.14, f32[]{:T(128)S(6)} %neg.16, ...), kind=kLoop, calls=%fused_computation.35 | loop fusion | flops 327680 | bytes 458792 | tf_op jit(solution)/shard_map/add | solution.py:72
  41.0 7.3 %multiply_add_fusion.22 = (f32[1,16384]{1,0:T(1,128)S(1)}, f32[1,16384]{1,0:T(1,128)S(1)}, f32[1,16384]{1,0:T(1,128)S(1)}, f32[1,16384]{1,0:T(1,128)S(1)}) fusion(f32[1,16384]{1,0:T(1,128)S(1)} %get-tuple-element.19, f32[1,16384]{1,0:T(1,128)S(1)} %get-tuple-element.20, f32[]{:T(128)} %bitcast.14, f32[]{:T(128)} %bitcast.10, f32[]{:T(128)} %bitcast.11, ...), kind=kLoop, calls=%fused_computation.34 | loop fusion | flops 294912 | bytes 655400 | tf_op jit(solution)/shard_map/add | solution.py:72
  48.3 2.6 multiply_add_fusion.19
  52.2 7.3 %multiply_add_fusion.17 = (f32[1,16384]{1,0:T(1,128)S(1)}, f32[1,16384]{1,0:T(1,128)S(1)}, f32[1,16384]{1,0:T(1,128)S(1)}, f32[1,16384]{1,0:T(1,128)S(1)}) fusion(f32[]{:T(128)} %bitcast.39, f32[]{:T(128)} %bitcast.35, f32[]{:T(128)} %bitcast.42, f32[3,16384]{1,0:T(4,128)} %param.10, f32[]{:T(128)} %bitcast.41, f32[]{:T(128)} %bitcast.40, f32[]{:T(128)S(6)} %neg.17, ...), kind=kLoop, calls=%fused_computation.29 | loop fusion | flops 327680 | bytes 458792 | tf_op jit(solution)/shard_map/add | solution.py:72
  59.4 7.3 %multiply_add_fusion.16 = (f32[1,16384]{1,0:T(1,128)S(1)}, f32[1,16384]{1,0:T(1,128)S(1)}, f32[1,16384]{1,0:T(1,128)S(1)}, f32[1,16384]{1,0:T(1,128)S(1)}) fusion(f32[1,16384]{1,0:T(1,128)S(1)} %get-tuple-element.25, f32[1,16384]{1,0:T(1,128)S(1)} %get-tuple-element.26, f32[]{:T(128)} %bitcast.40, f32[]{:T(128)} %bitcast.36, f32[]{:T(128)} %bitcast.37, ...), kind=kLoop, calls=%fused_computation.28 | loop fusion | flops 294912 | bytes 655400 | tf_op jit(solution)/shard_map/add | solution.py:72
  66.7 2.6 multiply_add_fusion.13
  70.7 7.4 %multiply_add_fusion.11 = (f32[1,16384]{1,0:T(1,128)S(1)}, f32[1,16384]{1,0:T(1,128)S(1)}, f32[1,16384]{1,0:T(1,128)S(1)}, f32[1,16384]{1,0:T(1,128)S(1)}) fusion(f32[]{:T(128)} %bitcast.58, f32[]{:T(128)} %bitcast.54, f32[]{:T(128)} %bitcast.61, f32[3,16384]{1,0:T(4,128)} %param.10, f32[]{:T(128)} %bitcast.60, f32[]{:T(128)} %bitcast.59, f32[]{:T(128)S(6)} %neg.18, ...), kind=kLoop, calls=%fused_computation.23 | loop fusion | flops 327680 | bytes 458792 | tf_op jit(solution)/shard_map/add | solution.py:72
  78.0 7.3 %multiply_add_fusion.10 = (f32[1,16384]{1,0:T(1,128)S(1)}, f32[1,16384]{1,0:T(1,128)S(1)}, f32[1,16384]{1,0:T(1,128)S(1)}, f32[1,16384]{1,0:T(1,128)S(1)}) fusion(f32[1,16384]{1,0:T(1,128)S(1)} %get-tuple-element.31, f32[1,16384]{1,0:T(1,128)S(1)} %get-tuple-element.32, f32[]{:T(128)} %bitcast.59, f32[]{:T(128)} %bitcast.55, f32[]{:T(128)} %bitcast.56, ...), kind=kLoop, calls=%fused_computation.22 | loop fusion | flops 294912 | bytes 655400 | tf_op jit(solution)/shard_map/add | solution.py:72
  85.3 2.6 multiply_add_fusion.7
  89.2 7.4 %multiply_add_fusion.5 = (f32[1,16384]{1,0:T(1,128)S(1)}, f32[1,16384]{1,0:T(1,128)S(1)}, f32[1,16384]{1,0:T(1,128)S(1)}, f32[1,16384]{1,0:T(1,128)S(1)}) fusion(f32[]{:T(128)} %bitcast.77, f32[]{:T(128)} %bitcast.73, f32[]{:T(128)} %bitcast.80, f32[3,16384]{1,0:T(4,128)} %param.10, f32[]{:T(128)} %bitcast.79, f32[]{:T(128)} %bitcast.78, f32[]{:T(128)S(6)} %neg.19, ...), kind=kLoop, calls=%fused_computation.17 | loop fusion | flops 327680 | bytes 458792 | tf_op jit(solution)/shard_map/add | solution.py:72
  96.5 7.4 %multiply_add_fusion.4 = (f32[1,16384]{1,0:T(1,128)S(1)}, f32[1,16384]{1,0:T(1,128)S(1)}, f32[1,16384]{1,0:T(1,128)S(1)}, f32[1,16384]{1,0:T(1,128)S(1)}) fusion(f32[1,16384]{1,0:T(1,128)S(1)} %get-tuple-element.37, f32[1,16384]{1,0:T(1,128)S(1)} %get-tuple-element.38, f32[]{:T(128)} %bitcast.78, f32[]{:T(128)} %bitcast.74, f32[]{:T(128)} %bitcast.75, ...), kind=kLoop, calls=%fused_computation.16 | loop fusion | flops 294912 | bytes 655400 | tf_op jit(solution)/shard_map/add | solution.py:72
  103.9 2.6 multiply_add_fusion.1
  113.3 5.3 %all-to-all-start = ((f32[8,1,32768]{2,1,0:T(1,128)}), f32[8,1,32768]{2,1,0:T(1,128)S(1)}, u32[]{:S(2)}, u32[]{:S(2)}) async-start(f32[8,1,32768]{2,1,0:T(1,128)} %broadcast_in_dim.24), calls=%async_computation | async-start | bytes 2097152 | tf_op jit(solution)/shard_map/all_to_all | solution.py:11
  124.9 8.7 %all-to-all-done = f32[8,1,32768]{2,1,0:T(1,128)S(1)} async-done(((f32[8,1,32768]{2,1,0:T(1,128)}), f32[8,1,32768]{2,1,0:T(1,128)S(1)}, u32[]{:S(2)}, u32[]{:S(2)}) %all-to-all-start) | async-done | bytes 1048608 | tf_op jit(solution)/shard_map/all_to_all | solution.py:11
  133.5 9.7 %all-to-all-start.2 = ((s32[1,32,4]{2,0,1:T(1,128)}), s32[1,32,4]{2,0,1:T(1,128)S(1)}, u32[]{:S(2)}, u32[]{:S(2)}) async-start(s32[1,32,4]{2,0,1:T(1,128)} %compare_select_fusion.1), calls=%async_computation.2 | async-start | bytes 32768 | tf_op jit(solution)/shard_map/all_to_all | solution.py:136
  144.1 21.5 %concatenate.8 = f32[61,16384]{1,0:T(8,128)} concatenate(f32[3,16384]{1,0:T(4,128)S(1)} %copy-done, f32[3,16384]{1,0:T(4,128)S(1)} %copy-done.2, f32[4,16384]{1,0:T(4,128)S(1)} %copy-done.1, f32[49,16384]{1,0:T(8,128)} %param.13, f32[1,16384]{1,0:T(1,128)S(1)} %bitcast.133, f32[1,16384]{1,0:T(1,128)S(1)} %bitcast.135), dimensions={0} | concatenate | bytes 7995392 | tf_op jit(solution)/shard_map/concatenate | solution.py:103
  165.6 6.9 %copy.48 = f32[16384,61]{1,0:T(8,128)} copy(f32[16384,61]{0,1:T(8,128)} %bitcast.130) | data formatting | bytes 7995392 | tf_op jit(solution)/shard_map/concatenate | solution.py:103
  172.5 44.3 %scatter_custom_fusion = f32[61,16384]{0,1:T(8,128)} fusion(s32[16384]{0:T(1024)} %get-tuple-element.75, f32[16384,61]{1,0:T(8,128)} %copy.48, f32[]{:T(128)} %constant.32.clone.1), kind=kCustom, calls=%fused_computation.3 | custom fusion | bytes 3998208 | tf_op jit(solution)/shard_map/scatter | solution.py:115
  216.9 7.7 %gather_fusion = f32[128,61,128]{1,2,0:T(8,128)} fusion(f32[61,128,128]{0,2,1:T(8,128)} %bitcast.129, s32[1024]{0:T(1024)S(1)} %pad_clamp_fusion), kind=kCustom, calls=%fused_computation | custom fusion | bytes 7995904 | tf_op jit(solution)/shard_map/gather | solution.py:124
  226.0 2.3 reshape.641
  228.3 9.1 %all-to-all-start.3 = ((f32[32,1,3904]{2,1,0:T(1,128)}), f32[32,1,3904]{2,1,0:T(1,128)S(1)}, u32[]{:S(2)}, u32[]{:S(2)}) async-start(f32[32,1,3904]{2,1,0:T(1,128)} %reshape.641), calls=%async_computation.3 | async-start | bytes 1015808 | tf_op jit(solution)/shard_map/all_to_all | solution.py:135
  238.8 11.3 %all-to-all-done.3 = f32[32,1,3904]{2,1,0:T(1,128)S(1)} async-done(((f32[32,1,3904]{2,1,0:T(1,128)}), f32[32,1,3904]{2,1,0:T(1,128)S(1)}, u32[]{:S(2)}, u32[]{:S(2)}) %all-to-all-start.3) | async-done | bytes 499744 | tf_op jit(solution)/shard_map/all_to_all | solution.py:135
  250.6 1.8 reduce.9
  254.0 4.5 %scatter_fusion = f32[61,128,16]{0,2,1:T(8,128)S(1)} fusion(f32[61,128,16]{0,2,1:T(8,128)S(1)} %broadcast_in_dim.44, s32[128]{0:T(128)S(1)} %fusion.4, f32[128,61,16]{1,2,0:T(8,128)S(1)} %bitcast.128), kind=kCustom, calls=%fused_computation.2 | custom fusion | bytes 1499648 | tf_op jit(solution)/shard_map/scatter | solution.py:142
  260.6 16.9 %all_to_all.31 = f32[32,1,1]{2,1,0:T(1,128)S(1)} all-to-all(f32[32,1,1]{2,1,0:T(1,128)S(1)} %broadcast_in_dim.51), channel_id=1, replica_groups=mesh['view'=8,'gauss'=32] {'gauss'}, dimensions={0} | all-to-all | bytes 256 | tf_op jit(solution)/shard_map/all_to_all | solution.py:11
  279.5 14.0 %all-gather.3.cloned.1.call-done = f32[488,128,16]{1,2,0:T(8,128)} async-done(((f32[61,128,16]{1,2,0:T(8,128)}), f32[488,128,16]{1,2,0:T(8,128)}) %all-gather.3.cloned.1.call-update) | async-done | bytes 3997712 | tf_op jit(solution)/shard_map/all_gather | solution.py:144
  293.6 9.3 %copy.50 = f32[61,128,8,16]{0,3,2,1:T(8,128)} copy(f32[61,128,8,16]{1,3,0,2:T(8,128)} %bitcast.131) | data formatting | bytes 7995392 | tf_op jit(solution)/shard_map/reshape | solution.py:144
  302.8 6.8 %copy.52 = f32[61,16384]{1,0:T(8,128)} copy(f32[61,16384]{0,1:T(8,128)} %bitcast.127) | data formatting | bytes 7995392
  (74 shorter events, 29.0 us)
Async XLA Ops:
  7.2 101.2 %copy-start.2 = (f32[3,16384]{1,0:T(4,128)S(1)}, f32[3,16384]{1,0:T(4,128)}, u32[]{:S(2)}) copy-start(f32[3,16384]{1,0:T(4,128)} %param.11) | copy-start | bytes 589828
  7.2 102.0 %copy-start.3 = (f32[4,2,16384]{2,1,0:T(2,128)S(1)}, f32[4,2,16384]{2,1,0:T(2,128)}, u32[]{:S(2)}) copy-start(f32[4,2,16384]{2,1,0:T(2,128)} %param.14) | copy-start | bytes 1572868
  12.3 99.5 %all-to-all-start.1 = ((s32[32,1,1]{2,1,0:T(1,128)}), s32[32,1,1]{2,1,0:T(1,128)S(1)}, u32[]{:S(2)}, u32[]{:S(2)}) async-start(s32[32,1,1]{2,1,0:T(1,128)} %broadcast_in_dim.45), calls=%async_computation.1 | async-start | bytes 32768 | tf_op jit(solution)/shard_map/all_to_all | solution.py:11
  24.3 119.7 %copy-start = (f32[3,16384]{1,0:T(4,128)S(1)}, f32[3,16384]{1,0:T(4,128)}, u32[]{:S(2)}) copy-start(f32[3,16384]{1,0:T(4,128)} %param.10) | copy-start | bytes 589828
  24.4 119.7 %copy-start.1 = (f32[4,16384]{1,0:T(4,128)S(1)}, f32[4,16384]{1,0:T(4,128)}, u32[]{:S(2)}) copy-start(f32[4,16384]{1,0:T(4,128)} %param.12) | copy-start | bytes 786436
  113.3 20.2 %all-to-all-start = ((f32[8,1,32768]{2,1,0:T(1,128)}), f32[8,1,32768]{2,1,0:T(1,128)S(1)}, u32[]{:S(2)}, u32[]{:S(2)}) async-start(f32[8,1,32768]{2,1,0:T(1,128)} %broadcast_in_dim.24), calls=%async_computation | async-start | bytes 2097152 | tf_op jit(solution)/shard_map/all_to_all | solution.py:11
  133.5 94.8 %all-to-all-start.2 = ((s32[1,32,4]{2,0,1:T(1,128)}), s32[1,32,4]{2,0,1:T(1,128)S(1)}, u32[]{:S(2)}, u32[]{:S(2)}) async-start(s32[1,32,4]{2,0,1:T(1,128)} %compare_select_fusion.1), calls=%async_computation.2 | async-start | bytes 32768 | tf_op jit(solution)/shard_map/all_to_all | solution.py:136
  228.3 21.8 %all-to-all-start.3 = ((f32[32,1,3904]{2,1,0:T(1,128)}), f32[32,1,3904]{2,1,0:T(1,128)S(1)}, u32[]{:S(2)}, u32[]{:S(2)}) async-start(f32[32,1,3904]{2,1,0:T(1,128)} %reshape.641), calls=%async_computation.3 | async-start | bytes 1015808 | tf_op jit(solution)/shard_map/all_to_all | solution.py:135
  237.4 56.2 %all-gather.3.cloned.1.call-start = ((), (), s32[]{:S(2)}) async-start(), calls=%async_computation.5 | async-start | bytes 4497408 | tf_op jit(solution)/shard_map/all_gather | solution.py:144
Sparse Core Ops, SparseCore 0:
  260.0 33.4 all-gather.2
